TPU v7x, 256 devices: a whole 4x4x8 slice. The times are simulated.
256 devices in a mesh: fsdp: 32 (over z_hi, x, core), tp: 8 (over y, z_lo).
Axes of the slice: x: 4, y: 4, z: 8 (z_hi: 4, z_lo: 2; z = z_hi * 2 + z_lo), core: 2. Of those that a mesh axis runs over, the one named last changes fastest.
Arguments:
- hidden: bfloat16 [8192, 8192], P('fsdp'), may hold values from -6 to 6
- norm_gain: float32 [8192], replicated, may hold values from 0.6 to 6, as said below
- w_query: bfloat16 [8192, 4096], P('fsdp', 'tp'), may hold values from -0.09375 to 0.09375
- w_key: bfloat16 [8192, 512], P('fsdp'), may hold values from -0.09375 to 0.09375
- w_value: bfloat16 [8192, 512], P('fsdp'), may hold values from -0.0625 to 0.0625
- bias_query: bfloat16 [4096], P('tp'), may hold values from -3 to 3
- bias_key: bfloat16 [512], replicated, may hold values from -3 to 3
- bias_value: bfloat16 [512], replicated, may hold values from -3 to 3
- w_out: bfloat16 [4096, 8192], P('tp', 'fsdp'), may hold values from -0.09375 to 0.09375
- seq_lengths: int32 [4], replicated, may hold values from 1 to 6144, 8192 in all
Outputs:
- hidden_out: float32 [8192, 8192], P(('fsdp', 'tp'))
Inputs may be any that keep to these rules, and one draw needn't show every extreme that they name: `seq_lengths`: 4 sequences packed in order; the lengths sum to 8192 and the longest has exactly 6144 tokens. `norm_gain`: positive gains.
All inputs are finite; a program needn't handle non-finite values.
Results may differ from a plain program's by a relative error of at most 0.014.
The roundings to bfloat16 on the way count: a program that leaves them out, or rounds other values in their place, can miss the bound.
Values may be sent and summed in bfloat16 or wider, within the bound.
No kernel may reach another device: no remote copies, remote signals or barrier semaphores. Data moves between devices by JAX's collectives and lax.ppermute only.
A program may use at most 128 MiB of HBM per device.

v0:
```python
import math
import jax
import jax.numpy as jnp
from jax import lax
from jax.sharding import Mesh
from jax.sharding import PartitionSpec as P

HEAD = 128
QHEADS = 32
KVHEADS = 4
TP = ("tp_0", "tp_1")
FSDP_TP = ("fsdp", "tp_0", "tp_1")
ROPE_BASE = 1000000.0
EPSILON = 1e-06
FLOOR = -1e30


def side_by_side(arrays, axis, dim, along):
    widths = [a.shape[along] for a in arrays]
    both = jnp.concatenate(arrays, axis=along)
    filled = lax.all_gather(both, axis, axis=dim, tiled=True)
    return tuple(jnp.split(filled, [sum(widths[:k]) for k in range(1, len(widths))], axis=along))


def scatter_axes(array, axes, dim):
    for axis in axes:
        array = lax.psum_scatter(array, axis, scatter_dimension=dim, tiled=True)
    return array


def token_layout(seq_lengths, token_index):
    seq_ends = jnp.cumsum(seq_lengths)
    seq_starts = seq_ends - seq_lengths
    member = (token_index[:, None] >= seq_ends[None, :]).astype(jnp.int32)
    segment = jnp.sum(member, axis=1)
    one_hot = segment[:, None] == jnp.arange(seq_lengths.shape[0], dtype=jnp.int32)[None, :]
    seq_begin = jnp.sum(jnp.where(one_hot, seq_starts[None, :], 0), axis=1)
    return (segment, token_index - seq_begin)


def rotary(vectors, position):
    half_size = vectors.shape[-1] // 2
    frequency = jnp.exp(
        jnp.arange(half_size, dtype=jnp.float32) * (-2.0 * math.log(ROPE_BASE) / vectors.shape[-1])
    )
    angle = position.astype(jnp.float32)[:, None] * frequency[None, :]
    cos_table = jnp.concatenate([jnp.cos(angle), jnp.cos(angle)], axis=1)[:, None, :]
    sin_table = jnp.concatenate([jnp.sin(angle), jnp.sin(angle)], axis=1)[:, None, :]
    turned = jnp.concatenate([-vectors[..., half_size:], vectors[..., :half_size]], axis=-1)
    return vectors * cos_table + turned * sin_table


def shards(
    hidden, norm_gain, w_query, w_key, w_value, bias_query, bias_key, bias_value, w_out, seq_lengths
):
    tok_rows = hidden.shape[0]
    first_row = lax.axis_index("fsdp") * tok_rows
    local_index = first_row + jnp.arange(tok_rows, dtype=jnp.int32)
    segment, position = token_layout(seq_lengths, local_index)
    widened = hidden.astype(jnp.float32)
    scale = lax.rsqrt(jnp.mean(widened * widened, axis=1, keepdims=True) + EPSILON)
    normed = (widened * scale * norm_gain[None, :]).astype(jnp.bfloat16)
    query_cols = w_query.shape[1]
    local_heads = query_cols // HEAD
    group_size = QHEADS // KVHEADS
    local_kv = max(local_heads // group_size, 1)
    first_kv = lax.axis_index(TP) * local_heads // group_size
    key_cols = local_kv * HEAD
    key_part = lax.dynamic_slice_in_dim(w_key, first_kv * HEAD, key_cols, 1)
    value_part = lax.dynamic_slice_in_dim(w_value, first_kv * HEAD, key_cols, 1)
    key_bias = lax.dynamic_slice_in_dim(bias_key, first_kv * HEAD, key_cols, 0)
    value_bias = lax.dynamic_slice_in_dim(bias_value, first_kv * HEAD, key_cols, 0)
    pieces = side_by_side((w_query, key_part, value_part), "fsdp", 0, 1)
    query, keys, values = tuple(
        (jnp.dot(normed, piece, preferred_element_type=jnp.float32) for piece in pieces)
    )
    query = rotary(
        (query + bias_query.astype(jnp.float32)[None, :]).reshape(tok_rows, -1, HEAD), position
    ).astype(jnp.bfloat16)
    keys = rotary(
        (keys + key_bias.astype(jnp.float32)[None, :]).reshape(tok_rows, -1, HEAD), position
    ).astype(jnp.bfloat16)
    values = (values + value_bias.astype(jnp.float32)[None, :]).astype(jnp.bfloat16)
    keys = keys.reshape(tok_rows, key_cols)
    per_kv = local_heads // local_kv
    query_grid = query.reshape(tok_rows, local_kv, per_kv, HEAD)
    start_state = (
        jnp.full((local_kv, per_kv, tok_rows), FLOOR, jnp.float32),
        jnp.zeros((local_kv, per_kv, tok_rows), jnp.float32),
        jnp.zeros((local_kv, per_kv, tok_rows, HEAD), jnp.float32),
    )
    key_piece, value_piece = side_by_side((keys, values), "fsdp", 0, 1)
    piece_rows = key_piece.shape[0]
    shard_count = max(piece_rows // tok_rows, 1)
    per_block = 1
    for divisor in range(1, 9):
        if shard_count % divisor == 0:
            per_block = divisor
    block_rows = min(per_block * tok_rows, piece_rows)
    block_count = piece_rows // block_rows

    def fold_block(block_number, carried):
        running_max, total, accumulated = carried
        offset = block_number * block_rows
        key_block = lax.dynamic_slice_in_dim(key_piece, offset, block_rows, 0).reshape(
            block_rows, local_kv, HEAD
        )
        value_block = lax.dynamic_slice_in_dim(value_piece, offset, block_rows, 0).reshape(
            block_rows, local_kv, HEAD
        )
        key_index = offset + jnp.arange(block_rows, dtype=jnp.int32)
        key_segment, unused = token_layout(seq_lengths, key_index)
        scores = jnp.einsum(
            "qkgd,nkd->kgqn", query_grid, key_block, preferred_element_type=jnp.float32
        ) * HEAD ** (-0.5)
        allowed = (
            (segment[:, None] == key_segment[None, :])
            & (local_index[:, None] >= key_index[None, :])
        )[None, None]
        scores = jnp.where(allowed, scores, FLOOR)
        new_max = jnp.maximum(running_max, jnp.max(scores, axis=3))
        weights = jnp.where(allowed, jnp.exp(scores - new_max[..., None]), 0.0)
        factor = jnp.exp(running_max - new_max)
        total = total * factor + jnp.sum(weights, axis=3)
        update = jnp.einsum(
            "kgqn,nkd->kgqd",
            weights.astype(jnp.bfloat16),
            value_block,
            preferred_element_type=jnp.float32,
        )
        accumulated = accumulated * factor[..., None] + update
        return (new_max, total, accumulated)

    final_state = lax.fori_loop(0, block_count, fold_block, start_state)
    mixed = final_state[2] / final_state[1][..., None]
    attended = jnp.transpose(mixed, (2, 0, 1, 3)).reshape(tok_rows, query_cols).astype(jnp.bfloat16)
    share_rows = tok_rows // lax.axis_size(TP)
    own_rows = lax.dynamic_slice_in_dim(
        hidden, lax.axis_index(TP) * share_rows, share_rows, 0
    ).astype(jnp.float32)
    terms = jnp.dot(
        attended,
        lax.all_gather(w_out, "fsdp", axis=1, tiled=True),
        preferred_element_type=jnp.float32,
    )
    summed = scatter_axes(terms.astype(jnp.bfloat16), TP, 0).astype(jnp.float32)
    return own_rows + summed


def solution(mesh):
    split = Mesh(mesh.devices.reshape(mesh.shape["fsdp"], 4, 2), ("fsdp", "tp_0", "tp_1"))
    return jax.shard_map(
        shards,
        mesh=split,
        in_specs=(
            P("fsdp", None),
            P(),
            P("fsdp", TP),
            P("fsdp", None),
            P("fsdp", None),
            P(TP),
            P(),
            P(),
            P(TP, "fsdp"),
            P(),
        ),
        out_specs=P(FSDP_TP, None),
        check_vma=False,
    )
```

profile of v0, /device:TPU:1, one launch (start us, length us, event | category | flops | bytes accessed | tf_op | source)
XLA Modules:
  0.0 359.9 jit_solution(5392411433781520436)
XLA Ops:
  6.5 0.9 constant_dynamic-slice_fusion
  7.4 1.7 pad_maximum_fusion
  9.2 0.8 reduce-window.9
  11.7 3.1 fusion.27
  15.1 91.3 %all-gather.4.cloned.1.call-done = bf16[8192,768]{1,0:T(8,128)(2,1)} async-done(((bf16[256,768]{1,0:T(8,128)(2,1)}), bf16[8192,768]{1,0:T(8,128)(2,1)}) %all-gather.4.cloned.1.call-update) | async-done | bytes 12582928 | tf_op jit(solution)/shard_map/all_gather | solution.py:21
  106.4 4.8 %fusion.39 = f32[256,128]{0,1:T(8,128)S(1)} fusion(bf16[8192,768]{1,0:T(8,128)(2,1)} %all-gather.4.cloned.1.call-done, f32[128]{0:T(128)S(1)} %get-tuple-element.345, bf16[256,8192]{1,0:T(8,128)(2,1)} %param.12, f32[8192]{0:T(1024)} %param.13, f32[256]{0:T(256)S(1)} %add_rsqrt_fusion), kind=kOutput, calls=%fused_computation.45 | convolution fusion | flops 545292288 | bytes 6456832 | tf_op jit(solution)/shard_map/dot_general | solution.py:75
  111.3 3.3 fusion.45
  116.5 7.0 %fusion.36 = f32[256,512]{1,0:T(8,128)S(1)} fusion(bf16[8192,768]{1,0:T(8,128)(2,1)} %all-gather.4.cloned.1.call-done, f32[512]{0:T(512)S(1)} %convert_element_type.88, bf16[256,8192]{1,0:T(8,128)(2,1)} %param.12, f32[8192]{0:T(1024)S(1)} %copy-done.3, f32[256]{0:T(256)S(1)} %add_rsqrt_fusion), kind=kOutput, calls=%fused_computation.44 | convolution fusion | flops 2156003328 | bytes 13143040 | tf_op jit(solution)/shard_map/dot_general | solution.py:75
  124.8 59.4 %all-gather.6.cloned.1.call-done = bf16[8192,256]{0,1:T(8,128)(2,1)} async-done(((bf16[256,256]{0,1:T(8,128)(2,1)}), bf16[8192,256]{0,1:T(8,128)(2,1)}) %all-gather.6.cloned.1.call-update) | async-done | bytes 4194320 | tf_op jit(solution)/shard_map/all_gather | solution.py:21
  184.2 4.0 %fusion.57 = (bf16[8192,128]{0,1:T(8,128)(2,1)S(1)}, bf16[8192,128]{0,1:T(8,128)(2,1)}) fusion(bf16[8192,256]{0,1:T(8,128)(2,1)} %all-gather.6.cloned.1.call-done), kind=kLoop, calls=%fused_computation.81 | loop fusion | bytes 8388608 | tf_op jit(solution)/shard_map/split | solution.py:22
  188.1 61.5 %while.20 = (s32[]{:T(128)}, f32[1,4,256]{2,1,0:T(4,128)S(1)}, f32[1,4,256]{2,1,0:T(4,128)S(1)}, f32[1,4,256,128]{3,2,1,0:T(8,128)S(1)}, s32[256]{0:T(256)S(1)},...) while((s32[]{:T(128)}, f32[1,4,256]{2,1,0:T(4,128)S(1)}, ...), condition=%wide.region_9.10_spmd.clone, body=%wide.region_5.9_spmd.clone.sunk | while | flops 1103001856 | bytes 63286520 | solution.py:134
  188.3 1.4 compare_and_fusion.2
  189.7 5.8 %fusion.69 = (f32[4,256]{1,0:T(4,128)S(1)}, f32[2048,256,4]{1,0,2:T(8,128)}) fusion(pred[256,2048]{0,1:T(8,128)(4,1)S(1)} %compare_and_fusion.2, bf16[256,1,4,128]{3,0,2,1:T(8,128)(2,1)S(1)} %get-tuple-element.450, bf16[8192,128]{0,1:T(8,128)(2,1)} %get-tuple-element.449, s32[]{:T(128)S(6)} %select_n.94), kind=kOutput, calls=%fused_computation.3.clone.1 | convolution fusion | flops 543161344 | bytes 9703428 | tf_op jit(solution)/shard_map/while/body/eval_jaxpr/qkgd,nkd->kgqn/dot_general | solution.py:113
  195.5 5.3 %fusion.72 = f32[1,4,256,128]{3,2,1,0:T(8,128)S(1)} fusion(f32[2048,256,4]{1,0,2:T(8,128)} %get-tuple-element.413, f32[4,256]{1,0:T(4,128)S(1)} %bitcast.99, pred[256,2048]{0,1:T(8,128)(4,1)S(1)} %compare_and_fusion.2, f32[1,4,256,128]{3,2,1,0:T(8,128)S(1)} %get-tuple-element.432, bf16[8192,128]{0,1:T(8,128)(2,1)S(1)} %get-tuple-element.451, ...), kind=kOutput, calls=%fused_computation.11.clone.1 | convolution fusion | flops 547749888 | bytes 10493957 | tf_op jit(solution)/shard_map/while/body/eval_jaxpr/kgqn,nkd->kgqd/dot_general | solution.py:125
  201.5 2.1 fusion.71
  203.8 1.4 compare_and_fusion.2
  205.2 5.8 %fusion.69 = (f32[4,256]{1,0:T(4,128)S(1)}, f32[2048,256,4]{1,0,2:T(8,128)}) fusion(pred[256,2048]{0,1:T(8,128)(4,1)S(1)} %compare_and_fusion.2, bf16[256,1,4,128]{3,0,2,1:T(8,128)(2,1)S(1)} %get-tuple-element.450, bf16[8192,128]{0,1:T(8,128)(2,1)} %get-tuple-element.449, s32[]{:T(128)S(6)} %select_n.94), kind=kOutput, calls=%fused_computation.3.clone.1 | convolution fusion | flops 543161344 | bytes 9703428 | tf_op jit(solution)/shard_map/while/body/eval_jaxpr/qkgd,nkd->kgqn/dot_general | solution.py:113
  211.0 5.1 %fusion.72 = f32[1,4,256,128]{3,2,1,0:T(8,128)S(1)} fusion(f32[2048,256,4]{1,0,2:T(8,128)} %get-tuple-element.413, f32[4,256]{1,0:T(4,128)S(1)} %bitcast.99, pred[256,2048]{0,1:T(8,128)(4,1)S(1)} %compare_and_fusion.2, f32[1,4,256,128]{3,2,1,0:T(8,128)S(1)} %get-tuple-element.432, bf16[8192,128]{0,1:T(8,128)(2,1)S(1)} %get-tuple-element.451, ...), kind=kOutput, calls=%fused_computation.11.clone.1 | convolution fusion | flops 547749888 | bytes 10493957 | tf_op jit(solution)/shard_map/while/body/eval_jaxpr/kgqn,nkd->kgqd/dot_general | solution.py:125
  216.8 2.1 fusion.71
  219.1 1.4 compare_and_fusion.2
  220.5 5.9 %fusion.69 = (f32[4,256]{1,0:T(4,128)S(1)}, f32[2048,256,4]{1,0,2:T(8,128)}) fusion(pred[256,2048]{0,1:T(8,128)(4,1)S(1)} %compare_and_fusion.2, bf16[256,1,4,128]{3,0,2,1:T(8,128)(2,1)S(1)} %get-tuple-element.450, bf16[8192,128]{0,1:T(8,128)(2,1)} %get-tuple-element.449, s32[]{:T(128)S(6)} %select_n.94), kind=kOutput, calls=%fused_computation.3.clone.1 | convolution fusion | flops 543161344 | bytes 9703428 | tf_op jit(solution)/shard_map/while/body/eval_jaxpr/qkgd,nkd->kgqn/dot_general | solution.py:113
  226.4 5.1 %fusion.72 = f32[1,4,256,128]{3,2,1,0:T(8,128)S(1)} fusion(f32[2048,256,4]{1,0,2:T(8,128)} %get-tuple-element.413, f32[4,256]{1,0:T(4,128)S(1)} %bitcast.99, pred[256,2048]{0,1:T(8,128)(4,1)S(1)} %compare_and_fusion.2, f32[1,4,256,128]{3,2,1,0:T(8,128)S(1)} %get-tuple-element.432, bf16[8192,128]{0,1:T(8,128)(2,1)S(1)} %get-tuple-element.451, ...), kind=kOutput, calls=%fused_computation.11.clone.1 | convolution fusion | flops 547749888 | bytes 10493957 | tf_op jit(solution)/shard_map/while/body/eval_jaxpr/kgqn,nkd->kgqd/dot_general | solution.py:125
  232.2 2.1 fusion.71
  234.5 1.4 compare_and_fusion.2
  235.9 5.8 %fusion.69 = (f32[4,256]{1,0:T(4,128)S(1)}, f32[2048,256,4]{1,0,2:T(8,128)}) fusion(pred[256,2048]{0,1:T(8,128)(4,1)S(1)} %compare_and_fusion.2, bf16[256,1,4,128]{3,0,2,1:T(8,128)(2,1)S(1)} %get-tuple-element.450, bf16[8192,128]{0,1:T(8,128)(2,1)} %get-tuple-element.449, s32[]{:T(128)S(6)} %select_n.94), kind=kOutput, calls=%fused_computation.3.clone.1 | convolution fusion | flops 543161344 | bytes 9703428 | tf_op jit(solution)/shard_map/while/body/eval_jaxpr/qkgd,nkd->kgqn/dot_general | solution.py:113
  241.7 5.1 %fusion.72 = f32[1,4,256,128]{3,2,1,0:T(8,128)S(1)} fusion(f32[2048,256,4]{1,0,2:T(8,128)} %get-tuple-element.413, f32[4,256]{1,0:T(4,128)S(1)} %bitcast.99, pred[256,2048]{0,1:T(8,128)(4,1)S(1)} %compare_and_fusion.2, f32[1,4,256,128]{3,2,1,0:T(8,128)S(1)} %get-tuple-element.432, bf16[8192,128]{0,1:T(8,128)(2,1)S(1)} %get-tuple-element.451, ...), kind=kOutput, calls=%fused_computation.11.clone.1 | convolution fusion | flops 547749888 | bytes 10493957 | tf_op jit(solution)/shard_map/while/body/eval_jaxpr/kgqn,nkd->kgqd/dot_general | solution.py:125
  247.6 2.1 fusion.71
  249.9 18.6 %all-gather.8.cloned.1.call-done = bf16[512,8192]{1,0:T(8,128)(2,1)} async-done(((bf16[512,256]{1,0:T(8,128)(2,1)}), bf16[512,8192]{1,0:T(8,128)(2,1)}) %all-gather.8.cloned.1.call-update) | async-done | bytes 8388624 | tf_op jit(solution)/shard_map/all_gather | solution.py:143
  268.6 7.7 %convolution_convert_fusion = bf16[256,8192]{1,0:T(8,128)(2,1)} fusion(bf16[256,512]{0,1:T(8,128)(2,1)S(1)} %bitcast.101, bf16[512,8192]{1,0:T(8,128)(2,1)} %all-gather.8.cloned.1.call-done), kind=kOutput, calls=%fused_computation.34 | convolution fusion | flops 2149580800 | bytes 12845056 | tf_op jit(solution)/shard_map/dot_general | solution.py:141
  276.3 47.2 %reduce-scatter.3.cloned.1.call-done = bf16[64,8192]{1,0:T(8,128)(2,1)} async-done(((bf16[256,8192]{1,0:T(8,128)(2,1)}), bf16[64,8192]{1,0:T(8,128)(2,1)}) %reduce-scatter.3.cloned.1.call-update) | async-done | bytes 1048592 | tf_op jit(solution)/shard_map/reduce_scatter | solution.py:27
  323.5 27.5 %reduce-scatter.5.cloned.1.call-done = bf16[32,8192]{1,0:T(8,128)(2,1)} async-done(((bf16[64,8192]{1,0:T(8,128)(2,1)}), bf16[32,8192]{1,0:T(8,128)(2,1)}) %reduce-scatter.5.cloned.1.call-update) | async-done | bytes 524304 | tf_op jit(solution)/shard_map/reduce_scatter | solution.py:27
  351.1 2.3 convert_add_fusion
  (77 shorter events, 8.7 us)
Async XLA Ops:
  6.5 99.9 %all-gather.4.cloned.1.call-start = ((), (), s32[]{:S(2)}) async-start(), calls=%async_computation.2 | async-start | bytes 12976128 | tf_op jit(solution)/shard_map/all_gather | solution.py:21
  6.5 104.7 %copy-start.3 = (f32[8192]{0:T(1024)S(1)}, f32[8192]{0:T(1024)}, u32[]{:S(2)}) copy-start(f32[8192]{0:T(1024)} %param.13) | copy-start | bytes 98308
  9.2 175.0 %all-gather.6.cloned.1.call-start = ((), (), s32[]{:S(2)}) async-start(), calls=%async_computation.3 | async-start | bytes 4325376 | tf_op jit(solution)/shard_map/all_gather | solution.py:21
  106.4 4.9 %copy-start.1 = (bf16[256,8192]{1,0:T(8,128)(2,1)S(1)}, bf16[256,8192]{1,0:T(8,128)(2,1)}, u32[]{:S(2)}) copy-start(bf16[256,8192]{1,0:T(8,128)(2,1)} %param.12) | copy-start | bytes 12582916
  106.4 9.9 %copy-start.2 = (bf16[512]{0:T(512)(128)(2,1)S(1)}, bf16[512]{0:T(512)(128)(2,1)}, u32[]{:S(2)}) copy-start(bf16[512]{0:T(512)(128)(2,1)} %param.17) | copy-start | bytes 3076
  106.4 9.9 %copy-start.4 = (s32[4]{0:T(128)S(1)}, s32[4]{0:T(128)}, u32[]{:S(2)}) copy-start(s32[4]{0:T(128)} %param.21) | copy-start | bytes 52
  115.3 153.2 %all-gather.8.cloned.1.call-start = ((), (), s32[]{:S(2)}) async-start(), calls=%async_computation.4 | async-start | bytes 8650752 | tf_op jit(solution)/shard_map/all_gather | solution.py:143
  116.1 207.4 %reduce-scatter.3.cloned.1.call-start = ((), (), s32[]{:S(2)}) async-start(), calls=%async_computation.5 | async-start | bytes 5242880 | tf_op jit(solution)/shard_map/reduce_scatter | solution.py:27
  195.5 6.0 %copy-start = (f32[2048,256,4]{1,0,2:T(8,128)S(1)}, f32[2048,256,4]{1,0,2:T(8,128)}, u32[]{:S(2)}) copy-start(f32[2048,256,4]{1,0,2:T(8,128)} %get-tuple-element.413) | copy-start | bytes 25165828 | tf_op jit(solution)/shard_map/while
  211.0 5.8 %copy-start = (f32[2048,256,4]{1,0,2:T(8,128)S(1)}, f32[2048,256,4]{1,0,2:T(8,128)}, u32[]{:S(2)}) copy-start(f32[2048,256,4]{1,0,2:T(8,128)} %get-tuple-element.413) | copy-start | bytes 25165828 | tf_op jit(solution)/shard_map/while
  226.4 5.8 %copy-start = (f32[2048,256,4]{1,0,2:T(8,128)S(1)}, f32[2048,256,4]{1,0,2:T(8,128)}, u32[]{:S(2)}) copy-start(f32[2048,256,4]{1,0,2:T(8,128)} %get-tuple-element.413) | copy-start | bytes 25165828 | tf_op jit(solution)/shard_map/while
  241.7 5.8 %copy-start = (f32[2048,256,4]{1,0,2:T(8,128)S(1)}, f32[2048,256,4]{1,0,2:T(8,128)}, u32[]{:S(2)}) copy-start(f32[2048,256,4]{1,0,2:T(8,128)} %get-tuple-element.413) | copy-start | bytes 25165828 | tf_op jit(solution)/shard_map/while
  276.3 74.8 %reduce-scatter.5.cloned.1.call-start = ((), (), s32[]{:S(2)}) async-start(), calls=%async_computation.6 | async-start | bytes 1572864 | tf_op jit(solution)/shard_map/reduce_scatter | solution.py:27
Sparse Core Ops, SparseCore 0:
  9.9 96.5 all-gather.3
  115.4 68.6 all-gather.5
  186.6 81.8 all-gather.7
  276.4 47.0 reduce-scatter.2
  325.9 25.1 reduce-scatter.4
where the time goes:
time: 360 us
  waiting for transfers between devices  245 us (68%)
  matrix products  66.7 us (19%)
  other arithmetic  25.7 us (7%)
  between operations  13.3 us (4%)
  local copies, waits for them, and re-layouts  8.8 us (2%)
    all_gather x2, waiting for transfers between devices, side_by_side(): filled = lax.all_gather(both, axis, axis=dim, tiled=True)  151 us
    reduce_scatter x2, waiting for transfers between devices, scatter_axes(): array = lax.psum_scatter(array, axis, scatter_dimension=dim, tiled=True)  74.7 us
    dot_general x4, matrix products, fold_block(): jnp.einsum('qkgd,nkd->kgqn', query_grid, key_block, preferred_element_typ...  23.2 us
    dot_general x4, matrix products, fold_block(): jnp.einsum('kgqn,nkd->kgqd', weights.astype(jnp.bfloat16), value_block, p...  20.7 us
    all_gather x1, waiting for transfers between devices, shards(): lax.all_gather(w_out, 'fsdp', axis=1, tiled=True)  18.6 us
    dot_general x3, matrix products, shards(): jnp.dot(normed, piece, preferred_element_type=jnp.float32)  15.1 us
    reduce_sum x4, other arithmetic, fold_block(): total = total * factor + jnp.sum(weights, axis=3)  8.28 us
    dot_general x1, matrix products, shards(): jnp.dot(attended, lax.all_gather(w_out, 'fsdp', axis=1, tiled=True), pref...  7.69 us
  transfers between devices with their start and end apart: 5, of which 5 were waited for; matrix products, arithmetic and copies ran while one was open for 21% of the time, Pallas kernels for 0%

commit v1 on v0

--- a/solution.py
+++ b/solution.py
@@ -13,6 +13,11 @@
 ROPE_BASE = 1000000.0
 EPSILON = 1e-06
 FLOOR = -1e30
+
+
+def swapped_in(block, axis, d):
+    repeated = jnp.stack([block] * lax.axis_size(axis))
+    return jnp.concatenate(lax.all_to_all(repeated, axis, 0, 0), axis=d)
 
 
 def side_by_side(arrays, axis, dim, along):
@@ -138,11 +143,7 @@
     own_rows = lax.dynamic_slice_in_dim(
         hidden, lax.axis_index(TP) * share_rows, share_rows, 0
     ).astype(jnp.float32)
-    terms = jnp.dot(
-        attended,
-        lax.all_gather(w_out, "fsdp", axis=1, tiled=True),
-        preferred_element_type=jnp.float32,
-    )
+    terms = jnp.dot(attended, swapped_in(w_out, "fsdp", 1), preferred_element_type=jnp.float32)
     summed = scatter_axes(terms.astype(jnp.bfloat16), TP, 0).astype(jnp.float32)
     return own_rows + summed
 

time: 360 us -> 471 us (1.31)
  waiting for transfers between devices: 245 us -> 363 us
  matrix products: 66.7 us -> 43.9 us
  starting transfers between devices: 0.35 us -> 13.4 us
    all_gather x2, waiting for transfers between devices: 151 us -> 255 us  [side_by_side(): filled = lax.all_gather(both, axis, axis=dim, tiled=True)]
    reduce_scatter x2, waiting for transfers between devices: 74.7 us -> 108 us  [scatter_axes(): array = lax.psum_scatter(array, axis, scatter_dimension=dim, tiled=True)]
    all_gather x1 -> x0, waiting for transfers between devices: 18.6 us -> none  [shards(): lax.all_gather(w_out, 'fsdp', axis=1, tiled=True)]
    all_to_all x0 -> x1, starting transfers between devices: none -> 13.3 us  [swapped_in(): return jnp.concatenate(lax.all_to_all(repeated, axis, 0, 0), axis=d)]
    dot_general x4, matrix products: 23.2 us -> 10.3 us  [fold_block(): jnp.einsum('qkgd,nkd->kgqn', query_grid, key_block, preferred_element_typ...]
    dot_general x4, matrix products: 20.7 us -> 10.7 us  [fold_block(): jnp.einsum('kgqn,nkd->kgqd', weights.astype(jnp.bfloat16), value_block, p...]
  transfers between devices with their start and end apart: 5 -> 5, of which waited for: 5 -> 4; matrix products, arithmetic and copies ran while one was open for 21% -> 12% of each run, Pallas kernels for 0% -> 0%
where the time goes in v1:
time: 471 us; the launch traced here: 470 us
  waiting for transfers between devices  363 us (77%)
  matrix products  43.9 us (9%)
  other arithmetic  25.8 us (5%)
  starting transfers between devices  13.4 us (3%)
  between operations  13.4 us (3%)
  local copies, waits for them, and re-layouts  10.3 us (2%)
    all_gather x2, waiting for transfers between devices, side_by_side(): filled = lax.all_gather(both, axis, axis=dim, tiled=True)  255 us
    reduce_scatter x2, waiting for transfers between devices, scatter_axes(): array = lax.psum_scatter(array, axis, scatter_dimension=dim, tiled=True)  108 us
    dot_general x3, matrix products, shards(): jnp.dot(normed, piece, preferred_element_type=jnp.float32)  15.2 us
    all_to_all x1, starting transfers between devices, swapped_in(): return jnp.concatenate(lax.all_to_all(repeated, axis, 0, 0), axis=d)  13.3 us
    dot_general x4, matrix products, fold_block(): jnp.einsum('kgqn,nkd->kgqd', weights.astype(jnp.bfloat16), value_block, p...  10.7 us
    dot_general x4, matrix products, fold_block(): jnp.einsum('qkgd,nkd->kgqn', query_grid, key_block, preferred_element_typ...  10.3 us
  transfers between devices with their start and end apart: 5, of which 4 were waited for; matrix products, arithmetic and copies ran while one was open for 12% of the time, Pallas kernels for 0%

profile of v1, /device:TPU:1, one launch (start us, length us, event | category | flops | bytes accessed | tf_op | source)
XLA Modules:
  0.0 470.1 jit_solution(3223049314585627442)
XLA Ops:
  6.5 0.9 constant_dynamic-slice_fusion
  7.4 1.7 pad_maximum_fusion
  11.7 3.1 fusion.27
  15.1 91.3 %all-gather.3.cloned.1.call-done = bf16[8192,768]{1,0:T(8,128)(2,1)} async-done(((bf16[256,768]{1,0:T(8,128)(2,1)}), bf16[8192,768]{1,0:T(8,128)(2,1)}) %all-gather.3.cloned.1.call-update) | async-done | bytes 12582928 | tf_op jit(solution)/shard_map/all_gather | solution.py:26
  106.4 4.8 %fusion.39 = f32[256,128]{0,1:T(8,128)S(1)} fusion(bf16[8192,768]{1,0:T(8,128)(2,1)} %all-gather.3.cloned.1.call-done, f32[128]{0:T(128)S(1)} %get-tuple-element.345, bf16[256,8192]{1,0:T(8,128)(2,1)} %param.12, f32[8192]{0:T(1024)} %param.13, f32[256]{0:T(256)S(1)} %add_rsqrt_fusion), kind=kOutput, calls=%fused_computation.45 | convolution fusion | flops 545292288 | bytes 6456832 | tf_op jit(solution)/shard_map/dot_general | solution.py:80
  111.3 3.3 fusion.45
  115.5 4.2 stack.2
  119.7 13.3 %all-to-all-start = ((bf16[32,512,256]{1,2,0:T(8,128)(2,1)}), bf16[32,512,256]{1,2,0:T(8,128)(2,1)}, u32[]{:S(2)}, u32[]{:S(2)}) async-start(bf16[32,512,256]{1,2,0:T(8,128)(2,1)} %stack.2), calls=%async_computation | async-start | bytes 16777216 | tf_op jit(solution)/shard_map/all_to_all | solution.py:20
  133.3 7.1 %fusion.36 = f32[256,512]{1,0:T(8,128)S(1)} fusion(bf16[8192,768]{1,0:T(8,128)(2,1)} %all-gather.3.cloned.1.call-done, f32[512]{0:T(512)S(1)} %convert_element_type.88, bf16[256,8192]{1,0:T(8,128)(2,1)} %param.12, f32[8192]{0:T(1024)S(1)} %copy-done.3, f32[256]{0:T(256)S(1)} %add_rsqrt_fusion), kind=kOutput, calls=%fused_computation.44 | convolution fusion | flops 2156003328 | bytes 13143040 | tf_op jit(solution)/shard_map/dot_general | solution.py:80
  141.6 163.4 %all-gather.5.cloned.1.call-done = bf16[8192,256]{0,1:T(8,128)(2,1)} async-done(((bf16[256,256]{0,1:T(8,128)(2,1)}), bf16[8192,256]{0,1:T(8,128)(2,1)}) %all-gather.5.cloned.1.call-update) | async-done | bytes 4194320 | tf_op jit(solution)/shard_map/all_gather | solution.py:26
  305.0 3.9 fusion.57
  308.9 35.9 %while.20 = (s32[]{:T(128)}, f32[1,4,256]{2,1,0:T(4,128)S(1)}, f32[1,4,256]{2,1,0:T(4,128)S(1)}, f32[1,4,256,128]{3,2,1,0:T(8,128)S(1)}, s32[256]{0:T(256)S(1)},...) while((s32[]{:T(128)}, f32[1,4,256]{2,1,0:T(4,128)S(1)}, ...), condition=%wide.region_9.10_spmd.clone, body=%wide.region_5.9_spmd.clone.sunk | while | flops 1103001856 | bytes 29732068 | solution.py:139
  309.1 1.4 compare_and_fusion.2
  310.5 2.6 fusion.69
  313.1 2.1 fusion.71
  315.2 2.7 fusion.72
  318.0 1.4 compare_and_fusion.2
  319.5 2.6 fusion.69
  322.1 2.1 fusion.71
  324.2 2.7 fusion.72
  327.0 1.4 compare_and_fusion.2
  328.5 2.6 fusion.69
  331.1 2.1 fusion.71
  333.2 2.7 fusion.72
  336.0 1.4 compare_and_fusion.2
  337.5 2.6 fusion.69
  340.1 2.1 fusion.71
  342.2 2.7 fusion.72
  345.2 7.7 %convolution_convert_fusion = bf16[256,8192]{1,0:T(8,128)(2,1)} fusion(bf16[256,512]{0,1:T(8,128)(2,1)S(1)} %bitcast.105, bf16[512,8192]{0,1:T(8,128)(2,1)} %bitcast.12), kind=kOutput, calls=%fused_computation.34 | convolution fusion | flops 2149580800 | bytes 12845056 | tf_op jit(solution)/shard_map/dot_general | solution.py:146
  353.0 80.8 %reduce-scatter.3.cloned.1.call-done = bf16[64,8192]{1,0:T(8,128)(2,1)} async-done(((bf16[256,8192]{1,0:T(8,128)(2,1)}), bf16[64,8192]{1,0:T(8,128)(2,1)}) %reduce-scatter.3.cloned.1.call-update) | async-done | bytes 1048592 | tf_op jit(solution)/shard_map/reduce_scatter | solution.py:32
  433.7 27.5 %reduce-scatter.5.cloned.1.call-done = bf16[32,8192]{1,0:T(8,128)(2,1)} async-done(((bf16[64,8192]{1,0:T(8,128)(2,1)}), bf16[32,8192]{1,0:T(8,128)(2,1)}) %reduce-scatter.5.cloned.1.call-update) | async-done | bytes 524304 | tf_op jit(solution)/shard_map/reduce_scatter | solution.py:32
  461.3 2.3 convert_add_fusion
  (72 shorter events, 6.0 us)
Async XLA Ops:
  6.5 99.9 %all-gather.3.cloned.1.call-start = ((), (), s32[]{:S(2)}) async-start(), calls=%async_computation.3 | async-start | bytes 12976128 | tf_op jit(solution)/shard_map/all_gather | solution.py:26
  6.5 104.7 %copy-start.3 = (f32[8192]{0:T(1024)S(1)}, f32[8192]{0:T(1024)}, u32[]{:S(2)}) copy-start(f32[8192]{0:T(1024)} %param.13) | copy-start | bytes 98308
  9.2 295.8 %all-gather.5.cloned.1.call-start = ((), (), s32[]{:S(2)}) async-start(), calls=%async_computation.4 | async-start | bytes 4325376 | tf_op jit(solution)/shard_map/all_gather | solution.py:26
  106.4 4.9 %copy-start = (bf16[256,8192]{1,0:T(8,128)(2,1)S(1)}, bf16[256,8192]{1,0:T(8,128)(2,1)}, u32[]{:S(2)}) copy-start(bf16[256,8192]{1,0:T(8,128)(2,1)} %param.12) | copy-start | bytes 12582916
  106.4 8.9 %copy-start.1 = (bf16[512,256]{1,0:T(8,128)(2,1)S(1)}, bf16[512,256]{1,0:T(8,128)(2,1)}, u32[]{:S(2)}) copy-start(bf16[512,256]{1,0:T(8,128)(2,1)} %param.20) | copy-start | bytes 786436
  119.7 13.4 %copy-start.4 = (s32[4]{0:T(128)S(1)}, s32[4]{0:T(128)}, u32[]{:S(2)}) copy-start(s32[4]{0:T(128)} %param.21) | copy-start | bytes 52
  119.7 13.5 %copy-start.2 = (bf16[512]{0:T(512)(128)(2,1)S(1)}, bf16[512]{0:T(512)(128)(2,1)}, u32[]{:S(2)}) copy-start(bf16[512]{0:T(512)(128)(2,1)} %param.17) | copy-start | bytes 3076
  119.7 225.4 %all-to-all-start = ((bf16[32,512,256]{1,2,0:T(8,128)(2,1)}), bf16[32,512,256]{1,2,0:T(8,128)(2,1)}, u32[]{:S(2)}, u32[]{:S(2)}) async-start(bf16[32,512,256]{1,2,0:T(8,128)(2,1)} %stack.2), calls=%async_computation | async-start | bytes 16777216 | tf_op jit(solution)/shard_map/all_to_all | solution.py:20
  133.0 300.7 %reduce-scatter.3.cloned.1.call-start = ((), (), s32[]{:S(2)}) async-start(), calls=%async_computation.5 | async-start | bytes 5242880 | tf_op jit(solution)/shard_map/reduce_scatter | solution.py:32
  352.9 108.4 %reduce-scatter.5.cloned.1.call-start = ((), (), s32[]{:S(2)}) async-start(), calls=%async_computation.6 | async-start | bytes 1572864 | tf_op jit(solution)/shard_map/reduce_scatter | solution.py:32
Sparse Core Ops, SparseCore 0:
  9.9 96.5 all-gather.2
  115.5 189.5 all-gather.4
  353.0 80.6 reduce-scatter.2
  436.1 25.1 reduce-scatter.4
